TPU v7x, 256 devices: a whole 4x4x8 slice. The times are simulated.
256 devices in a mesh: dp: 2 (over x_lo), expert: 128 (over y, z, x_hi, core).
Axes of the slice: x: 4 (x_hi: 2, x_lo: 2; x = x_hi * 2 + x_lo), y: 4, z: 8, core: 2. Of those that a mesh axis runs over, the one named last changes fastest.
Arguments:
- tokens: bfloat16 [256, 256, 1280], P(('dp', 'expert')), may hold values from -12 to 12
- router: bfloat16 [1280, 128], replicated, may hold values from -3 to 3
- w_in: bfloat16 [128, 1280, 5120], P('expert', None, 'dp'), may hold values from -0.15625 to 0.15625
- b_in: bfloat16 [128, 5120], P('expert'), may hold values from -3 to 3
- w_out: bfloat16 [128, 5120, 1280], P('expert', 'dp'), may hold values from -0.078125 to 0.078125
- b_out: bfloat16 [128, 1280], P('expert'), may hold values from -3 to 3
Outputs:
- mixed: bfloat16 [256, 256, 1280], P(('dp', 'expert'))
All inputs are finite; a program needn't handle non-finite values.
Results may differ from a plain program's by a relative error of at most 0.014.
Values may be sent and summed in bfloat16 or wider, within the bound.
No kernel may reach another device: no remote copies, remote signals or barrier semaphores. Data moves between devices by JAX's collectives and lax.ppermute only.
A program may use at most 64 MiB of HBM per device.

v0:
```python
import jax
import jax.numpy as jnp
from jax import lax
from jax.sharding import Mesh
from jax.sharding import PartitionSpec as P

EXPERT = ("expert_0", "expert_1", "expert_2", "expert_3")
DP_EXPERT = ("dp", "expert_0", "expert_1", "expert_2", "expert_3")


def sent_to_all(shard, axis):
    copies = jnp.broadcast_to(shard, (lax.axis_size(axis), *shard.shape))
    return lax.all_to_all(copies, axis, split_axis=0, concat_axis=0, tiled=True)


def in_order(pieces, dim):
    pieces = jnp.moveaxis(pieces, 0, dim)
    dims = pieces.shape
    return pieces.reshape(*dims[:dim], dims[dim] * dims[dim + 1], *dims[dim + 2 :])


def gather_directly(shard, axis, dim):
    pieces = sent_to_all(shard, axis)
    return in_order(pieces, dim)


def in_blocks(shard, dim, count):
    dims = shard.shape
    pieces = shard.reshape(*dims[:dim], count, dims[dim] // count, *dims[dim + 1 :])
    return jnp.moveaxis(pieces, dim, 0)


def sent_and_summed(shard, axis, dim):
    pieces = in_blocks(shard, dim, lax.axis_size(axis))
    arrived = lax.all_to_all(pieces, axis, split_axis=0, concat_axis=0, tiled=True)
    return arrived.astype(jnp.float32).sum(axis=0)


def exchange_in_order(pieces, axes, turns):
    dims = [lax.axis_size(a) for a in axes]
    pieces = pieces.reshape(*dims, *pieces.shape[1:])
    for k in turns:
        pieces = lax.all_to_all(pieces, axes[k], split_axis=k, concat_axis=k, tiled=True)
    return pieces.reshape(-1, *pieces.shape[len(axes) :])


def two_step_exchange(shard, groups, turns, split_dim, concat_dim):
    count = lax.axis_size(groups[0]) * lax.axis_size(groups[1])
    pieces = in_blocks(shard, split_dim, count)
    return in_order(exchange_in_order(pieces, groups, turns), concat_dim)


def shards(tokens, router, w_in, b_in, w_out, b_out):
    logits = jnp.einsum("bmd,de->bme", tokens, router, preferred_element_type=jnp.float32)
    dispatch = jax.nn.softmax(logits, axis=1).astype(jnp.bfloat16)
    combine = jax.nn.softmax(logits, axis=2).astype(jnp.bfloat16)
    slot_inputs = jnp.einsum(
        "bme,bmd->ebd", dispatch, tokens, preferred_element_type=jnp.float32
    ).astype(jnp.bfloat16)
    width = tokens.shape[2]
    arrived = lax.all_to_all(slot_inputs, EXPERT, split_axis=0, concat_axis=0, tiled=True)
    sources = arrived.shape[0]
    images = arrived.shape[1]
    paired = gather_directly(arrived, "dp", 0)
    flat = paired.reshape(paired.shape[0] * images, width)
    half = w_in.shape[2]
    offset = lax.axis_index("dp") * half
    bias_half = lax.dynamic_slice_in_dim(b_in[0], offset, half, 0).astype(jnp.float32)
    hidden = jax.nn.gelu(
        jnp.dot(flat, w_in[0], preferred_element_type=jnp.float32) + bias_half, approximate=False
    ).astype(jnp.bfloat16)
    summed = sent_and_summed(
        jnp.dot(hidden, w_out[0], preferred_element_type=jnp.float32).astype(jnp.bfloat16), "dp", 0
    )
    result = (summed + b_out[0].astype(jnp.float32)).astype(jnp.bfloat16)
    shaped = result.reshape(sources, images, width)
    returned = two_step_exchange(
        shaped, (("expert_0", "expert_1", "expert_2"), "expert_3"), (1, 0), 0, 0
    )
    mixed = jnp.einsum("bme,ebd->bmd", combine, returned, preferred_element_type=jnp.float32)
    return mixed.astype(jnp.bfloat16)


def solution(mesh):
    finer = Mesh(
        mesh.devices.reshape(mesh.shape["dp"], 4, 8, 2, 2),
        ("dp", "expert_0", "expert_1", "expert_2", "expert_3"),
    )
    return jax.shard_map(
        shards,
        mesh=finer,
        in_specs=(
            P(DP_EXPERT, None, None),
            P(),
            P(EXPERT, None, "dp"),
            P(EXPERT, None),
            P(EXPERT, "dp", None),
            P(EXPERT, None),
        ),
        out_specs=P(DP_EXPERT, None, None),
        check_vma=False,
    )
```

profile of v0, /device:TPU:1, one launch (start us, length us, event | category | flops | bytes accessed | tf_op | source)
XLA Modules:
  0.0 103.0 jit_solution(1009964734027190072)
XLA Ops:
  0.0 0.0 copy-start
  0.0 1.1 %copy-done = bf16[1,256,1280]{2,1,0:T(8,128)(2,1)S(1)} copy-done((bf16[1,256,1280]{2,1,0:T(8,128)(2,1)S(1)}, bf16[1,256,1280]{2,1,0:T(8,128)(2,1)}, u32[]{:S(2)}) %copy-start) | copy-done | bytes 655384
  1.1 1.4 %fusion.97 = (f32[256]{0:T(256)S(1)}, f32[128]{0:T(128)S(1)}, f32[256,128]{1,0:T(8,128)S(1)}) fusion(bf16[1280,128]{1,0:T(8,128)(2,1)} %param.7, bf16[1,256,1280]{2,1,0:T(8,128)(2,1)S(1)} %copy-done), kind=kOutput, calls=%fused_computation.108 | convolution fusion | flops 83951232 | bytes 1115648 | tf_op jit(solution)/shard_map/bmd,de->bme/dot_general | solution.py:54
  2.5 0.2 fusion.61
  2.7 0.3 fusion.21
  3.0 0.5 broadcast.35
  3.5 0.8 reduce.12
  4.3 0.1 reshape.77
  4.4 0.0 copy-start.1
  4.4 33.2 %all_to_all.28 = bf16[128,2,640]{2,1,0:T(2,128)(2,1)S(1)} all-to-all(bf16[128,2,640]{2,1,0:T(2,128)(2,1)S(1)} %reshape.77), channel_id=1, replica_groups=mesh['dp'=2,'expert_0'=4,'expert_1'=8,'expert_2'=2,'expert_3'=2] {'exper..., dimensions={0} | all-to-all | bytes 655360 | tf_op jit(solution)/shard_map/all_to_all | solution.py:61
  37.6 0.3 reshape.78
  37.9 0.9 broadcast_in_dim.2
  38.8 3.5 %all-to-all-start.1 = ((bf16[2,128,1,1280]{3,1,2,0:T(8,128)(2,1)}), bf16[2,128,1,1280]{3,1,2,0:T(8,128)(2,1)S(1)}, u32[]{:S(2)}, u32[]{:S(2)}) async-start(bf16[2,128,1,1280]{3,1,2,0:T(8,128)(2,1)} %broadcast_in_dim.2), calls=%async_computation.1 | async-start | bytes 1310720 | tf_op jit(solution)/shard_map/all_to_all | solution.py:13
  42.4 0.0 copy-done.1
  42.4 9.3 %all-to-all-done.1 = bf16[2,128,1,1280]{3,1,2,0:T(8,128)(2,1)S(1)} async-done(((bf16[2,128,1,1280]{3,1,2,0:T(8,128)(2,1)}), bf16[2,128,1,1280]{3,1,2,0:T(8,128)(2,1)S(1)}, u32[]{:S(2)}, u32[]{:S(2)}) %all-to-all-start.1) | async-done | bytes 655392 | tf_op jit(solution)/shard_map/all_to_all | solution.py:13
  51.7 0.0 copy-start.2
  51.7 14.1 %fusion.17 = bf16[256,1280]{1,0:T(8,128)(2,1)} fusion(bf16[1,2560,1280]{2,1,0:T(8,128)(2,1)} %param.10, bf16[256,1280]{1,0:T(8,128)(2,1)S(1)} %bitcast.40, bf16[1,1280,2560]{2,1,0:T(8,128)(2,1)} %param.8, f32[2560]{0:T(1024)S(1)} %convert_reduce_fusion.1), kind=kOutput, calls=%fused_computation.24 | convolution fusion | flops 3399024640 | bytes 14428160 | tf_op jit(solution)/shard_map/dot_general | solution.py:73
  65.8 3.5 %all-to-all-start.2 = ((bf16[2,128,1280]{2,1,0:T(8,128)(2,1)}), bf16[2,128,1280]{2,1,0:T(8,128)(2,1)S(1)}, u32[]{:S(2)}, u32[]{:S(2)}) async-start(bf16[2,128,1280]{2,1,0:T(8,128)(2,1)} %bitcast.7), calls=%async_computation.2 | async-start | bytes 1310720 | tf_op jit(solution)/shard_map/all_to_all | solution.py:35
  69.3 0.0 copy-done.2
  69.3 8.4 %all-to-all-done.2 = bf16[2,128,1280]{2,1,0:T(8,128)(2,1)S(1)} async-done(((bf16[2,128,1280]{2,1,0:T(8,128)(2,1)}), bf16[2,128,1280]{2,1,0:T(8,128)(2,1)S(1)}, u32[]{:S(2)}, u32[]{:S(2)}) %all-to-all-start.2) | async-done | bytes 655392 | tf_op jit(solution)/shard_map/all_to_all | solution.py:35
  77.8 0.1 convert_reduce_fusion
  77.9 0.4 reduce_sum.32
  78.3 5.5 %all_to_all.29 = bf16[64,2,1,1,1280]{4,0,3,2,1:T(8,128)(2,1)S(1)} all-to-all(bf16[64,2,1,1,1280]{4,0,3,2,1:T(8,128)(2,1)S(1)} %fusion.60), channel_id=1, replica_groups=mesh['dp'=2,'expert_0'=4,'expert_1'=8,'expert_2'=2,'expert_3'=2] {'exper..., dimensions={1} | all-to-all | bytes 655360 | tf_op jit(solution)/shard_map/all_to_all | solution.py:43
  83.8 0.3 copy.14
  84.1 17.5 %all_to_all.30 = bf16[64,2,1,1,1280]{4,1,3,2,0:T(2,128)(2,1)S(1)} all-to-all(bf16[64,2,1,1,1280]{4,1,3,2,0:T(2,128)(2,1)S(1)} %copy.14), channel_id=1, replica_groups=mesh['dp'=2,'expert_0'=4,'expert_1'=8,'expert_2'=2,'expert_3'=2] {'exper..., dimensions={0} | all-to-all | bytes 655360 | tf_op jit(solution)/shard_map/all_to_all | solution.py:43
  101.6 0.1 reshape.72
  101.8 1.2 %fusion.20 = bf16[1,256,1280]{2,1,0:T(8,128)(2,1)} fusion(bf16[128,1280]{1,0:T(8,128)(2,1)S(1)} %reshape.72, f32[256,128]{1,0:T(8,128)S(1)} %get-tuple-element.9, f32[256]{0:T(256)S(1)} %get-tuple-element.5, f32[256]{0:T(256)S(1)} %get-tuple-element.7), kind=kOutput, calls=%fused_computation.26 | convolution fusion | flops 84312064 | bytes 1116160 | tf_op jit(solution)/shard_map/bme,ebd->bmd/dot_general | solution.py:80
  (4 shorter events, 0.1 us)
Async XLA Ops:
  0.0 1.1 %copy-start = (bf16[1,256,1280]{2,1,0:T(8,128)(2,1)S(1)}, bf16[1,256,1280]{2,1,0:T(8,128)(2,1)}, u32[]{:S(2)}) copy-start(bf16[1,256,1280]{2,1,0:T(8,128)(2,1)} %param.6) | copy-start | bytes 1966084
  4.4 38.0 %copy-start.1 = (bf16[1,5120]{1,0:T(2,128)(2,1)S(1)}, bf16[1,5120]{1,0:T(2,128)(2,1)}, u32[]{:S(2)}) copy-start(bf16[1,5120]{1,0:T(2,128)(2,1)} %param.9) | copy-start | bytes 30724
  38.8 12.9 %all-to-all-start.1 = ((bf16[2,128,1,1280]{3,1,2,0:T(8,128)(2,1)}), bf16[2,128,1,1280]{3,1,2,0:T(8,128)(2,1)S(1)}, u32[]{:S(2)}, u32[]{:S(2)}) async-start(bf16[2,128,1,1280]{3,1,2,0:T(8,128)(2,1)} %broadcast_in_dim.2), calls=%async_computation.1 | async-start | bytes 1310720 | tf_op jit(solution)/shard_map/all_to_all | solution.py:13
  51.7 17.6 %copy-start.2 = (bf16[1,1280]{1,0:T(2,128)(2,1)S(1)}, bf16[1,1280]{1,0:T(2,128)(2,1)}, u32[]{:S(2)}) copy-start(bf16[1,1280]{1,0:T(2,128)(2,1)} %param.11) | copy-start | bytes 7684
  65.8 12.0 %all-to-all-start.2 = ((bf16[2,128,1280]{2,1,0:T(8,128)(2,1)}), bf16[2,128,1280]{2,1,0:T(8,128)(2,1)S(1)}, u32[]{:S(2)}, u32[]{:S(2)}) async-start(bf16[2,128,1280]{2,1,0:T(8,128)(2,1)} %bitcast.7), calls=%async_computation.2 | async-start | bytes 1310720 | tf_op jit(solution)/shard_map/all_to_all | solution.py:35
where the time goes:
time: 103 us
  blocking collectives  56.2 us (55%)
  waiting for transfers between devices  17.7 us (17%)
  matrix products  17 us (17%)
  starting transfers between devices  7.02 us (7%)
  local copies, waits for them, and re-layouts  3.72 us (4%)
  other arithmetic  1.24 us (1%)
    all_to_all x1, blocking collectives, shards(): lax.all_to_all(slot_inputs, EXPERT, split_axis=0, concat_axis=0, tiled=True)  33.2 us
    all_to_all x2, blocking collectives, exchange_in_order(): lax.all_to_all(pieces, axes[k], split_axis=k, concat_axis=k, tiled=True)  22.9 us
    dot_general x1, matrix products, shards(): jnp.dot(hidden, w_out[0], preferred_element_type=jnp.float32)  14.1 us
    all_to_all x1, waiting for transfers between devices, sent_to_all(): return lax.all_to_all(copies, axis, split_axis=0, concat_axis=0, tiled=True)  9.29 us
    all_to_all x1, waiting for transfers between devices, sent_and_summed(): lax.all_to_all(pieces, axis, split_axis=0, concat_axis=0, tiled=True)  8.45 us
    all_to_all x1, starting transfers between devices, sent_to_all(): return lax.all_to_all(copies, axis, split_axis=0, concat_axis=0, tiled=True)  3.51 us
    all_to_all x1, starting transfers between devices, sent_and_summed(): lax.all_to_all(pieces, axis, split_axis=0, concat_axis=0, tiled=True)  3.51 us
  transfers between devices with their start and end apart: 2, of which 2 were waited for; matrix products, arithmetic and copies ran while one was open for 0% of the time, Pallas kernels for 0%

commit v1 on v0

v1 whole, which is shorter than its diff:
```python
import functools
import math

import jax
import jax.numpy as jnp
from jax import lax
from jax.experimental import pallas as pl
from jax.experimental.pallas import tpu as pltpu
from jax.sharding import Mesh
from jax.sharding import PartitionSpec as P

EXPERT = ("expert",)
ALL = ("dp", "expert")
CHUNK = 512


def front_kernel(x_hbm, r_hbm, slots_ref, comb_ref, x_ref, r_ref, sems):
    cx = pltpu.make_async_copy(x_hbm, x_ref, sems.at[0])
    cr = pltpu.make_async_copy(r_hbm, r_ref, sems.at[1])
    cx.start()
    cr.start()
    cx.wait()
    cr.wait()
    x = x_ref[...]
    logits = jnp.dot(x, r_ref[...], preferred_element_type=jnp.float32)
    top = jnp.max(logits, axis=0, keepdims=True)
    ex = jnp.exp(logits - top)
    dispatch = (ex / jnp.sum(ex, axis=0, keepdims=True)).astype(jnp.bfloat16)
    slots_ref[...] = lax.dot_general(
        dispatch, x, (((0,), (0,)), ((), ())), preferred_element_type=jnp.float32
    ).astype(jnp.bfloat16)
    top = jnp.max(logits, axis=1, keepdims=True)
    ex = jnp.exp(logits - top)
    comb_ref[...] = (ex / jnp.sum(ex, axis=1, keepdims=True)).astype(jnp.bfloat16)


def front(x, router):
    tokens, width = x.shape
    experts = router.shape[1]
    return pl.pallas_call(
        front_kernel,
        out_shape=(
            jax.ShapeDtypeStruct((experts, width), jnp.bfloat16),
            jax.ShapeDtypeStruct((tokens, experts), jnp.bfloat16),
        ),
        in_specs=[pl.BlockSpec(memory_space=pl.ANY)] * 2,
        out_specs=(pl.BlockSpec(memory_space=pltpu.VMEM),) * 2,
        scratch_shapes=[
            pltpu.VMEM(x.shape, x.dtype),
            pltpu.VMEM(router.shape, router.dtype),
            pltpu.SemaphoreType.DMA((2,)),
        ],
        name="front",
    )(x, router)


def mlp_kernel(x_ref, bi_ref, bo_ref, wi_hbm, wo_hbm, o_ref, wi, wo, acc, si, so):
    hid = wi.shape[1]
    n = hid // CHUNK
    half = lax.axis_index("dp")

    def copy_in(j):
        cols = pl.ds(j * CHUNK, CHUNK)
        return pltpu.make_async_copy(wi_hbm.at[:, cols], wi.at[:, cols], si.at[j])

    def copy_out(j):
        rows = pl.ds(j * CHUNK, CHUNK)
        return pltpu.make_async_copy(wo_hbm.at[rows, :], wo.at[rows, :], so.at[j])

    for j in range(n):
        copy_in(j).start()
        copy_out(j).start()
    bias = bi_ref[...].astype(jnp.float32)
    bias = jnp.where(half == 0, bias[:, :hid], bias[:, hid:])
    x = x_ref[...]

    def first(j):
        copy_in(j).wait()
        cols = pl.ds(j * CHUNK, CHUNK)
        return jnp.dot(x, wi[:, cols], preferred_element_type=jnp.float32)

    pre = first(0)
    for j in range(n):
        v = pre + bias[:, j * CHUNK : (j + 1) * CHUNK]
        if j + 1 < n:
            pre = first(j + 1)
        hidden = (v * (1.0 + lax.erf(v * (1.0 / math.sqrt(2.0)))) * 0.5).astype(jnp.bfloat16)
        copy_out(j).wait()
        part = jnp.dot(
            hidden, wo[pl.ds(j * CHUNK, CHUNK), :], preferred_element_type=jnp.float32
        )
        if j == 0:
            share = bo_ref[...].astype(jnp.float32)
            share = jnp.where(half == 0, share, jnp.zeros_like(share))
            acc[...] = part + share
        elif j + 1 < n:
            acc[...] += part
        else:
            o_ref[...] = (acc[...] + part).astype(jnp.bfloat16)


def mlp(x, w_in, b_in, w_out, b_out):
    rows, width = x.shape
    hid = w_in.shape[1]
    n = hid // CHUNK
    vmem = pl.BlockSpec(memory_space=pltpu.VMEM)
    hbm = pl.BlockSpec(memory_space=pl.ANY)
    return pl.pallas_call(
        mlp_kernel,
        out_shape=jax.ShapeDtypeStruct((rows, width), jnp.bfloat16),
        in_specs=[vmem, vmem, vmem, hbm, hbm],
        out_specs=vmem,
        scratch_shapes=[
            pltpu.VMEM(w_in.shape, w_in.dtype),
            pltpu.VMEM(w_out.shape, w_out.dtype),
            pltpu.VMEM((rows, width), jnp.float32),
            pltpu.SemaphoreType.DMA((n,)),
            pltpu.SemaphoreType.DMA((n,)),
        ],
        name="mlp",
    )(x, b_in, b_out, w_in, w_out)


def exchange(rows):
    count, width = rows.shape
    pieces = rows.reshape(count, 2, width // 2)
    pieces = lax.all_to_all(pieces, ALL, split_axis=0, concat_axis=0, tiled=True)
    return pieces.reshape(count, width)


def shards(tokens, router, w_in, b_in, w_out, b_out):
    slots, combine = front(tokens[0], router)
    arrived = exchange(jnp.concatenate([slots, slots], axis=0))
    share = mlp(arrived, w_in[0], b_in, w_out[0], b_out)
    returned = exchange(share)
    weights = jnp.concatenate([combine, combine], axis=1)
    mixed = jnp.dot(weights, returned, preferred_element_type=jnp.float32)
    return mixed.astype(jnp.bfloat16)[None]


def solution(mesh):
    return jax.shard_map(
        shards,
        mesh=mesh,
        in_specs=(
            P(ALL, None, None),
            P(),
            P("expert", None, "dp"),
            P("expert", None),
            P("expert", "dp", None),
            P("expert", None),
        ),
        out_specs=P(ALL, None, None),
        check_vma=False,
    )
```

time: 103 us -> 84.5 us (0.82)
  waiting for transfers between devices: 17.7 us -> 0 us
  matrix products: 17 us -> 1.18 us
  Pallas kernels: 0 us -> 11.9 us
  blocking collectives: 56.2 us -> 67 us
  starting transfers between devices: 7.02 us -> 0 us
    all_to_all x2 -> x0, waiting for transfers between devices: 17.7 us -> none  [the longest x1 9.29 us: sent_to_all(): return lax.all_to_all(copies, axis, split_axis=0, concat_axis=0, tiled=True)]
    dot_general x4 -> x1, matrix products: 17 us -> 1.18 us  [shards(): mixed = jnp.dot(weights, returned, preferred_element_type=jnp.float32)]
    pallas_call x0 -> x2, Pallas kernels: none -> 11.9 us  [the longest x1 9.27 us: mlp(): pl.pallas_call(mlp_kernel, out_shape=jax.ShapeDtypeStruct((rows, width),...]
    all_to_all x3 -> x2, blocking collectives: 56.2 us -> 67 us  [exchange(): lax.all_to_all(pieces, ALL, split_axis=0, concat_axis=0, tiled=True)]
    all_to_all x2 -> x0, starting transfers between devices: 7.02 us -> none  [the longest x1 3.51 us: sent_to_all(): return lax.all_to_all(copies, axis, split_axis=0, concat_axis=0, tiled=True)]
    reshape x0 -> x2, local copies, waits for them, and re-layouts: none -> 2.05 us  [exchange(): pieces = rows.reshape(count, 2, width // 2)]
    concatenate x0 -> x1, other arithmetic: none -> 1.12 us  [shards(): arrived = exchange(jnp.concatenate([slots, slots], axis=0))]
  transfers between devices with their start and end apart: 2 -> 0, of which waited for: 2 -> 0; matrix products, arithmetic and copies ran while one was open for 0% -> 0% of each run, Pallas kernels for 0% -> 0%
where the time goes in v1:
time: 84.5 us; the launch traced here: 84.2 us
  blocking collectives  67 us (79%)
  Pallas kernels  11.9 us (14%)
  local copies, waits for them, and re-layouts  3.04 us (4%)
  matrix products  1.18 us (1%)
  other arithmetic  1.12 us (1%)
    all_to_all x2, blocking collectives, exchange(): lax.all_to_all(pieces, ALL, split_axis=0, concat_axis=0, tiled=True)  67 us
    pallas_call x1, Pallas kernels, mlp(): pl.pallas_call(mlp_kernel, out_shape=jax.ShapeDtypeStruct((rows, width),...  9.27 us
    pallas_call x1, Pallas kernels, front(): pl.pallas_call(front_kernel, out_shape=(jax.ShapeDtypeStruct((experts, wi...  2.61 us
    reshape x2, local copies, waits for them, and re-layouts, exchange(): pieces = rows.reshape(count, 2, width // 2)  2.05 us

profile of v1, /device:TPU:1, one launch (start us, length us, event | category | flops | bytes accessed | tf_op | source)
XLA Modules:
  0.0 84.2 jit_solution(312135344297027114)
XLA Ops:
  0.0 2.6 %front.1 = (bf16[128,1280]{1,0:T(8,128)(2,1)}, bf16[256,128]{1,0:T(8,128)(2,1)}) custom-call(bf16[256,1280]{1,0:T(8,128)(2,1)} %bitcast.16, bf16[1280,128]{1,0:T(8,128)(2,1)} %r_hbm.1), custom_call_target="tpu_custom_call" | custom-call | tf_op jit(solution)/shard_map/front/pallas_call | solution.py:40
  2.6 1.1 %pad_maximum_fusion = bf16[256,1280]{1,0:T(8,128)(2,1)S(1)} fusion(bf16[128,1280]{1,0:T(8,128)(2,1)} %get-tuple-element.8), kind=kLoop, calls=%fused_computation.2 | loop fusion | flops 1310720 | bytes 983040 | tf_op jit(solution)/shard_map/concatenate | solution.py:133
  3.7 0.1 reshape.12
  3.9 38.1 %all_to_all.10 = bf16[256,2,640]{2,1,0:T(2,128)(2,1)S(1)} all-to-all(bf16[256,2,640]{2,1,0:T(2,128)(2,1)S(1)} %reshape.12), channel_id=1, replica_groups=mesh['dp'=2,'expert'=128] {'dp','expert'}, dimensions={0} | all-to-all | bytes 1310720 | tf_op jit(solution)/shard_map/all_to_all | solution.py:127
  42.0 0.9 %copy.7 = bf16[32,8,2,640]{3,1,2,0:T(8,128)(2,1)} copy(bf16[32,8,2,640]{3,2,1,0:T(2,128)(2,1)S(1)} %bitcast.13) | data formatting | bytes 1310720
  42.9 9.3 %mlp.1 = bf16[256,1280]{1,0:T(8,128)(2,1)} custom-call(bf16[256,1280]{1,0:T(8,128)(2,1)} %bitcast.15, bf16[1,5120]{1,0:T(2,128)(2,1)} %bi_ref.1, bf16[1,1280]{1,0:T(2,128)(2,1)} %bo_ref.1, bf16[1280,2560]{1,0:T(8,128)(2,1)} %bitcast.10, bf16[2560,1280]{1,0:T(8,128)(2,1)} %bitcast.11), custom_call_target="tpu_custom_call" | custom-call | tf_op jit(solution)/shard_map/mlp/pallas_call | solution.py:108
  52.2 1.9 %reshape.14 = bf16[256,2,640]{2,1,0:T(2,128)(2,1)S(1)} reshape(bf16[256,1280]{1,0:T(8,128)(2,1)} %mlp.1) | data formatting | bytes 1310720 | tf_op jit(solution)/shard_map/reshape | solution.py:126
  54.1 0.0 copy-start
  54.1 28.9 %all_to_all.11 = bf16[256,2,640]{2,1,0:T(2,128)(2,1)S(1)} all-to-all(bf16[256,2,640]{2,1,0:T(2,128)(2,1)S(1)} %reshape.14), channel_id=1, replica_groups=mesh['dp'=2,'expert'=128] {'dp','expert'}, dimensions={0} | all-to-all | bytes 1310720 | tf_op jit(solution)/shard_map/all_to_all | solution.py:127
  83.0 0.1 copy.8
  83.1 0.0 copy-done
  83.1 1.2 %fusion = bf16[1,256,1280]{2,1,0:T(8,128)(2,1)} fusion(bf16[256,1280]{1,0:T(8,128)(2,1)S(1)} %bitcast.12, bf16[256,128]{1,0:T(8,128)(2,1)S(1)} %copy-done), kind=kOutput, calls=%fused_computation.1 | convolution fusion | flops 168361984 | bytes 1376256 | tf_op jit(solution)/shard_map/dot_general | solution.py:137
Async XLA Ops:
  54.1 29.0 %copy-start = (bf16[256,128]{1,0:T(8,128)(2,1)S(1)}, bf16[256,128]{1,0:T(8,128)(2,1)}, u32[]{:S(2)}) copy-start(bf16[256,128]{1,0:T(8,128)(2,1)} %get-tuple-element.7) | copy-start | bytes 196612

commit v2 on v1

v2 whole, which is shorter than its diff:
```python
import functools
import math

import jax
import jax.numpy as jnp
from jax import lax
from jax.experimental import pallas as pl
from jax.experimental.pallas import tpu as pltpu
from jax.sharding import Mesh
from jax.sharding import PartitionSpec as P

EXPERT = ("expert",)
ALL = ("dp", "expert")
CHUNK = 512
AHEAD = CHUNK
FLIGHT = 4


def in_hbm(array):
    return pltpu.with_memory_space_constraint(array, pltpu.HBM)


def front_kernel(
    x_hbm, r_hbm, wi_hbm, bi_hbm, bo_hbm, slots_ref, comb_ref, ahead_ref, bias_ref, share_ref,
    x_ref, r_ref, bi_ref, bo_ref, sems,
):
    experts = r_ref.shape[1]
    half = lax.axis_index("dp")
    hid = bias_ref.shape[1]
    cx = pltpu.make_async_copy(x_hbm, x_ref, sems.at[0])
    cr = pltpu.make_async_copy(r_hbm, r_ref, sems.at[1])
    cw = pltpu.make_async_copy(wi_hbm.at[:, pl.ds(0, AHEAD)], ahead_ref, sems.at[2])
    ci = pltpu.make_async_copy(bi_hbm, bi_ref, sems.at[3])
    co = pltpu.make_async_copy(bo_hbm, bo_ref, sems.at[4])
    cx.start()
    cr.start()
    ci.start()
    co.start()
    cw.start()
    cx.wait()
    cr.wait()
    x = x_ref[...]
    logits = jnp.dot(x, r_ref[...], preferred_element_type=jnp.float32)
    top = jnp.max(logits, axis=0, keepdims=True)
    ex = jnp.exp(logits - top)
    dispatch = (ex / jnp.sum(ex, axis=0, keepdims=True)).astype(jnp.bfloat16)
    slots = lax.dot_general(
        dispatch, x, (((0,), (0,)), ((), ())), preferred_element_type=jnp.float32
    ).astype(jnp.bfloat16)
    slots_ref[:experts, :] = slots
    slots_ref[experts:, :] = slots
    top = jnp.max(logits, axis=1, keepdims=True)
    ex = jnp.exp(logits - top)
    combine = (ex / jnp.sum(ex, axis=1, keepdims=True)).astype(jnp.bfloat16)
    comb_ref[:, :experts] = combine
    comb_ref[:, experts:] = combine
    ci.wait()
    co.wait()
    bias = bi_ref[...].astype(jnp.float32)
    bias_ref[...] = jnp.where(half == 0, bias[:, :hid], bias[:, hid:])
    share = bo_ref[...].astype(jnp.float32)
    share_ref[...] = jnp.where(half == 0, share, jnp.zeros_like(share))
    cw.wait()


def front(x, router, w_in, b_in, b_out):
    tokens, width = x.shape
    experts = router.shape[1]
    return pl.pallas_call(
        front_kernel,
        out_shape=(
            jax.ShapeDtypeStruct((2 * experts, width), jnp.bfloat16),
            jax.ShapeDtypeStruct((tokens, 2 * experts), jnp.bfloat16),
            jax.ShapeDtypeStruct((width, AHEAD), jnp.bfloat16),
            jax.ShapeDtypeStruct((1, w_in.shape[1]), jnp.float32),
            jax.ShapeDtypeStruct(b_out.shape, jnp.float32),
        ),
        in_specs=[pl.BlockSpec(memory_space=pltpu.HBM)] * 5,
        out_specs=(pl.BlockSpec(memory_space=pltpu.VMEM),) * 5,
        scratch_shapes=[
            pltpu.VMEM(x.shape, x.dtype),
            pltpu.VMEM(router.shape, router.dtype),
            pltpu.VMEM(b_in.shape, b_in.dtype),
            pltpu.VMEM(b_out.shape, b_out.dtype),
            pltpu.SemaphoreType.DMA((5,)),
        ],
        compiler_params=pltpu.CompilerParams(vmem_limit_bytes=8 << 20),
        name="front",
    )(in_hbm(x), in_hbm(router), in_hbm(w_in), in_hbm(b_in), in_hbm(b_out))


def mlp_kernel(x_ref, ahead_ref, bias_ref, share_ref, wi_hbm, wo_hbm, o_ref, wi, wo, acc, si, so):
    n = wi.shape[1] // CHUNK

    def copy_in(j):
        cols = pl.ds(j * CHUNK, CHUNK)
        return pltpu.make_async_copy(wi_hbm.at[:, cols], wi.at[:, cols], si.at[j])

    def copy_out(j):
        rows = pl.ds(j * CHUNK, CHUNK)
        return pltpu.make_async_copy(wo_hbm.at[rows, :], wo.at[rows, :], so.at[j])

    copies = [copy_out(0)]
    for j in range(1, n):
        copies += [copy_in(j), copy_out(j)]
    for copy in copies[:FLIGHT]:
        copy.start()

    def wait(k):
        copies[k].wait()
        if k + FLIGHT < len(copies):
            copies[k + FLIGHT].start()

    x = x_ref[...]
    pre = jnp.dot(x, ahead_ref[...], preferred_element_type=jnp.float32)
    for j in range(n):
        cols = pl.ds(j * CHUNK, CHUNK)
        v = pre + bias_ref[:, cols]
        hidden = (v * (1.0 + lax.erf(v * (1.0 / math.sqrt(2.0)))) * 0.5).astype(jnp.bfloat16)
        wait(2 * j)
        if j + 1 < n:
            wait(2 * j + 1)
            pre = jnp.dot(
                x, wi[:, pl.ds((j + 1) * CHUNK, CHUNK)], preferred_element_type=jnp.float32
            )
        part = jnp.dot(hidden, wo[cols, :], preferred_element_type=jnp.float32)
        if j == 0:
            acc[...] = part + share_ref[...]
        elif j + 1 < n:
            acc[...] += part
        else:
            o_ref[...] = (acc[...] + part).astype(jnp.bfloat16)


def mlp(x, ahead, bias, share, w_in, w_out):
    rows, width = x.shape
    n = w_in.shape[1] // CHUNK
    vmem = pl.BlockSpec(memory_space=pltpu.VMEM)
    hbm = pl.BlockSpec(memory_space=pltpu.HBM)
    return pl.pallas_call(
        mlp_kernel,
        out_shape=jax.ShapeDtypeStruct((rows, width), jnp.bfloat16),
        in_specs=[vmem, vmem, vmem, vmem, hbm, hbm],
        out_specs=vmem,
        scratch_shapes=[
            pltpu.VMEM(w_in.shape, w_in.dtype),
            pltpu.VMEM(w_out.shape, w_out.dtype),
            pltpu.VMEM((rows, width), jnp.float32),
            pltpu.SemaphoreType.DMA((n,)),
            pltpu.SemaphoreType.DMA((n,)),
        ],
        compiler_params=pltpu.CompilerParams(vmem_limit_bytes=24 << 20),
        name="mlp",
    )(x, ahead, bias, share, in_hbm(w_in), in_hbm(w_out))


def exchange(rows):
    count, width = rows.shape
    pieces = rows.reshape(count, 2, width // 2)
    pieces = lax.all_to_all(pieces, ALL, split_axis=0, concat_axis=0, tiled=True)
    return pieces.reshape(count, width)


def shards(tokens, router, w_in, b_in, w_out, b_out):
    slots, weights, ahead, bias, share = front(tokens[0], router, w_in[0], b_in, b_out)
    arrived = exchange(slots)
    share = mlp(arrived, ahead, bias, share, w_in[0], w_out[0])
    returned = exchange(share)
    mixed = jnp.dot(weights, returned, preferred_element_type=jnp.float32)
    return mixed.astype(jnp.bfloat16)[None]


def solution(mesh):
    return jax.shard_map(
        shards,
        mesh=mesh,
        in_specs=(
            P(ALL, None, None),
            P(),
            P("expert", None, "dp"),
            P("expert", None),
            P("expert", "dp", None),
            P("expert", None),
        ),
        out_specs=P(ALL, None, None),
        check_vma=False,
    )
```

time: 84.5 us -> 76.9 us (0.910)
  Pallas kernels: 11.9 us -> 8.27 us
  local copies, waits for them, and re-layouts: 3.04 us -> 0.45 us
  other arithmetic: 1.12 us -> 0 us
    pallas_call x1, Pallas kernels: 9.27 us -> 6.35 us  [mlp(): pl.pallas_call(mlp_kernel, out_shape=jax.ShapeDtypeStruct((rows, width),...]
    reshape x2, local copies, waits for them, and re-layouts: 2.05 us -> 0.3 us  [exchange(): pieces = rows.reshape(count, 2, width // 2)]
    concatenate x1 -> x0, other arithmetic: 1.12 us -> none  [shards(): arrived = exchange(jnp.concatenate([slots, slots], axis=0))]
where the time goes in v2:
time: 76.9 us; the launch traced here: 76.8 us
  blocking collectives  66.8 us (87%)
  Pallas kernels  8.27 us (11%)
  matrix products  1.18 us (2%)
    all_to_all x2, blocking collectives, exchange(): lax.all_to_all(pieces, ALL, split_axis=0, concat_axis=0, tiled=True)  66.8 us
    pallas_call x1, Pallas kernels, mlp(): pl.pallas_call(mlp_kernel, out_shape=jax.ShapeDtypeStruct((rows, width),...  6.35 us
    pallas_call x1, Pallas kernels, front(): pl.pallas_call(front_kernel, out_shape=(jax.ShapeDtypeStruct((2 * experts...  1.93 us

profile of v2, /device:TPU:1, one launch (start us, length us, event | category | flops | bytes accessed | tf_op | source)
XLA Modules:
  0.0 76.8 jit_solution(17684731865931735995)
XLA Ops:
  0.0 1.9 %front.1 = (bf16[256,1280]{1,0:T(8,128)(2,1)S(1)}, bf16[256,256]{1,0:T(8,128)(2,1)S(1)}, bf16[1280,512]{1,0:T(8,128)(2,1)S(1)}, f32[1,2560]{1,0:T(1,128)S(1)}, f32[1,1280]{1,0:T(1,128)S(1)}) custom-call(bf16[256,1280]{1,0:T(8,128)(2,1)} %bitcast.18, bf16[1280,128]{1,0:T(8,128)(2,1)} %r_hbm.1, bf16[1280,2560]{1,0:T(8,128)(2,1)} %bitcast.12, ...), custom_call_target="tpu_custom_call" | custom-call | tf_op jit(solution)/shard_map/front/pallas_call | solution.py:69
  1.9 0.1 reshape.12
  2.1 38.1 %all_to_all.10 = bf16[256,2,640]{2,1,0:T(2,128)(2,1)S(1)} all-to-all(bf16[256,2,640]{2,1,0:T(2,128)(2,1)S(1)} %reshape.12), channel_id=1, replica_groups=mesh['dp'=2,'expert'=128] {'dp','expert'}, dimensions={0} | all-to-all | bytes 1310720 | tf_op jit(solution)/shard_map/all_to_all | solution.py:160
  40.2 0.1 copy.7
  40.3 6.3 %mlp.1 = bf16[256,1280]{1,0:T(8,128)(2,1)S(1)} custom-call(bf16[256,1280]{1,0:T(8,128)(2,1)S(1)} %bitcast.11, bf16[1280,512]{1,0:T(8,128)(2,1)S(1)} %get-tuple-element.12.ahead_ref, f32[1,2560]{1,0:T(1,128)S(1)} %get-tuple-element.13.bias_ref, f32[1,1280]{1,0:T(1,128)S(1)} %get-tuple-element.14.share_ref, bf16[1280,2560]{1,0:T(8,128)(2,1)} %bitcast.13, ...), custom_call_target="tpu_custom_call" | custom-call | tf_op jit(solution)/shard_map/mlp/pallas_call | solution.py:140
  46.6 0.1 reshape.14
  46.8 28.8 %all_to_all.11 = bf16[256,2,640]{2,1,0:T(2,128)(2,1)S(1)} all-to-all(bf16[256,2,640]{2,1,0:T(2,128)(2,1)S(1)} %reshape.14), channel_id=1, replica_groups=mesh['dp'=2,'expert'=128] {'dp','expert'}, dimensions={0} | all-to-all | bytes 1310720 | tf_op jit(solution)/shard_map/all_to_all | solution.py:160
  75.5 0.1 copy.8
  75.6 1.2 %fusion = bf16[1,256,1280]{2,1,0:T(8,128)(2,1)} fusion(bf16[256,256]{1,0:T(8,128)(2,1)S(1)} %get-tuple-element.10, bf16[256,1280]{1,0:T(8,128)(2,1)S(1)} %bitcast.15), kind=kOutput, calls=%fused_computation.1 | convolution fusion | flops 168099840 | bytes 1441792 | tf_op jit(solution)/shard_map/dot_general | solution.py:169

commit v3 on v2

v3 whole, which is shorter than its diff:
```python
import functools
import math

import jax
import jax.numpy as jnp
from jax import lax
from jax.experimental import pallas as pl
from jax.experimental.pallas import tpu as pltpu
from jax.sharding import Mesh
from jax.sharding import PartitionSpec as P

EXPERT = ("expert",)
ALL = ("dp", "expert")
CHUNK = 512
GRANT = 8 << 20
PARTS = 2
HOLD_FLOPS = 20_000_000_000
HOLD_BYTES = 64 << 20


def in_hbm(array):
    return pltpu.with_memory_space_constraint(array, pltpu.HBM)


def front_kernel(
    x_hbm, r_hbm, bi_hbm, bo_hbm, slots_ref, comb_ref, bias_ref, share_ref,
    x_ref, r_ref, bi_ref, bo_ref, sems,
):
    experts = r_ref.shape[1]
    half = lax.axis_index("dp")
    hid = bias_ref.shape[1]
    cx = pltpu.make_async_copy(x_hbm, x_ref, sems.at[0])
    cr = pltpu.make_async_copy(r_hbm, r_ref, sems.at[1])
    ci = pltpu.make_async_copy(bi_hbm, bi_ref, sems.at[2])
    co = pltpu.make_async_copy(bo_hbm, bo_ref, sems.at[3])
    cx.start()
    cr.start()
    ci.start()
    co.start()
    cx.wait()
    cr.wait()
    x = x_ref[...]
    logits = jnp.dot(x, r_ref[...], preferred_element_type=jnp.float32)
    top = jnp.max(logits, axis=0, keepdims=True)
    ex = jnp.exp(logits - top)
    dispatch = (ex / jnp.sum(ex, axis=0, keepdims=True)).astype(jnp.bfloat16)
    slots = lax.dot_general(
        dispatch, x, (((0,), (0,)), ((), ())), preferred_element_type=jnp.float32
    )
    width = slots.shape[1]
    slots = slots.astype(jnp.bfloat16).reshape(experts, 2, width // 2)
    slots_ref[:experts] = slots
    slots_ref[experts:] = slots
    top = jnp.max(logits, axis=1, keepdims=True)
    ex = jnp.exp(logits - top)
    combine = (ex / jnp.sum(ex, axis=1, keepdims=True)).astype(jnp.bfloat16)
    comb_ref[:, :experts] = combine
    comb_ref[:, experts:] = combine
    ci.wait()
    co.wait()
    bias = bi_ref[...].astype(jnp.float32)
    bias_ref[...] = jnp.where(half == 0, bias[:, :hid], bias[:, hid:])
    share = bo_ref[...].astype(jnp.float32)
    share_ref[...] = jnp.where(half == 0, share, jnp.zeros_like(share))


def front(x, router, b_in, b_out, hid):
    tokens, width = x.shape
    experts = router.shape[1]
    return pl.pallas_call(
        front_kernel,
        out_shape=(
            jax.ShapeDtypeStruct((2 * experts, 2, width // 2), jnp.bfloat16),
            jax.ShapeDtypeStruct((tokens, 2 * experts), jnp.bfloat16),
            jax.ShapeDtypeStruct((1, hid), jnp.float32),
            jax.ShapeDtypeStruct(b_out.shape, jnp.float32),
        ),
        in_specs=[pl.BlockSpec(memory_space=pltpu.HBM)] * 4,
        out_specs=(pl.BlockSpec(memory_space=pltpu.VMEM),) * 4,
        scratch_shapes=[
            pltpu.VMEM(x.shape, x.dtype),
            pltpu.VMEM(router.shape, router.dtype),
            pltpu.VMEM(b_in.shape, b_in.dtype),
            pltpu.VMEM(b_out.shape, b_out.dtype),
            pltpu.SemaphoreType.DMA((4,)),
        ],
        compiler_params=pltpu.CompilerParams(vmem_limit_bytes=8 << 20),
        name="front",
    )(in_hbm(x), in_hbm(router), in_hbm(b_in), in_hbm(b_out))


def mlp_kernel(x_ref, bias_ref, share_ref, wi, wo, o_ref, hid):
    x = x_ref[...]
    for j in range(wi.shape[1] // CHUNK):
        cols = pl.ds(j * CHUNK, CHUNK)
        v = jnp.dot(x, wi[:, cols], preferred_element_type=jnp.float32) + bias_ref[:, cols]
        hid[:, cols] = (v * (1.0 + lax.erf(v * (1.0 / math.sqrt(2.0)))) * 0.5).astype(jnp.bfloat16)
    part = jnp.dot(hid[...], wo[...], preferred_element_type=jnp.float32)
    o_ref[...] = (part + share_ref[...]).astype(jnp.bfloat16)


def mlp(x, bias, share, w_in, w_out):
    rows, width = x.shape
    vmem = pl.BlockSpec(memory_space=pltpu.VMEM)
    return pl.pallas_call(
        mlp_kernel,
        out_shape=jax.ShapeDtypeStruct((rows, width), jnp.bfloat16),
        in_specs=[vmem] * 5,
        out_specs=vmem,
        scratch_shapes=[pltpu.VMEM((rows, w_in.shape[1]), jnp.bfloat16)],
        compiler_params=pltpu.CompilerParams(vmem_limit_bytes=GRANT),
        name="mlp",
    )(x, bias, share, w_in, w_out)


def hold_kernel(x_ref, o_ref):
    pass


def hold(x):
    vmem = pl.BlockSpec(memory_space=pltpu.VMEM)
    return pl.pallas_call(
        hold_kernel,
        out_shape=jax.ShapeDtypeStruct(x.shape, x.dtype),
        in_specs=[vmem],
        out_specs=vmem,
        input_output_aliases={0: 0},
        compiler_params=pltpu.CompilerParams(vmem_limit_bytes=1 << 20),
        cost_estimate=pl.CostEstimate(
            flops=HOLD_FLOPS, bytes_accessed=HOLD_BYTES, transcendentals=0
        ),
        name="hold",
    )(x)


def mix_kernel(w_ref, r_ref, o_hbm, out, sems):
    rows = out.shape[0] // PARTS
    copies = []
    for i in range(PARTS):
        part = pl.ds(i * rows, rows)
        out[part, :] = jnp.dot(
            w_ref[part, :], r_ref[...], preferred_element_type=jnp.float32
        ).astype(jnp.bfloat16)
        copies.append(pltpu.make_async_copy(out.at[part, :], o_hbm.at[part, :], sems.at[i]))
        copies[-1].start()
    for copy in copies:
        copy.wait()


def mix(weights, returned):
    shape = (weights.shape[0], returned.shape[1])
    vmem = pl.BlockSpec(memory_space=pltpu.VMEM)
    return pl.pallas_call(
        mix_kernel,
        out_shape=jax.ShapeDtypeStruct(shape, jnp.bfloat16),
        in_specs=[vmem, vmem],
        out_specs=pl.BlockSpec(memory_space=pltpu.HBM),
        scratch_shapes=[pltpu.VMEM(shape, jnp.bfloat16), pltpu.SemaphoreType.DMA((PARTS,))],
        compiler_params=pltpu.CompilerParams(vmem_limit_bytes=8 << 20),
        name="mix",
    )(weights, returned)


def exchange(pieces):
    count = pieces.shape[0]
    pieces = lax.all_to_all(pieces, ALL, split_axis=0, concat_axis=0, tiled=True)
    return pieces.reshape(count, -1)


def shards(tokens, router, w_in, b_in, w_out, b_out):
    slots, weights, bias, share = front(tokens[0], router, b_in, b_out, w_in.shape[2])
    arrived = exchange(hold(hold(slots)))
    share = mlp(arrived, bias, share, w_in[0], w_out[0])
    returned = exchange(share.reshape(share.shape[0], 2, -1))
    return mix(weights, returned)[None]


def solution(mesh):
    return jax.shard_map(
        shards,
        mesh=mesh,
        in_specs=(
            P(ALL, None, None),
            P(),
            P("expert", None, "dp"),
            P("expert", None),
            P("expert", "dp", None),
            P("expert", None),
        ),
        out_specs=P(ALL, None, None),
        check_vma=False,
    )
```

time: 76.9 us -> 74.4 us (0.967)
  Pallas kernels: 8.27 us -> 7 us
  matrix products: 1.18 us -> 0 us
    pallas_call x1, Pallas kernels: 6.35 us -> 3.72 us  [mlp(): pl.pallas_call(mlp_kernel, out_shape=jax.ShapeDtypeStruct((rows, width),...]
    dot_general x1 -> x0, matrix products: 1.18 us -> none  [shards(): mixed = jnp.dot(weights, returned, preferred_element_type=jnp.float32)]
    pallas_call x0 -> x3, Pallas kernels: none -> 1.13 us  [the longest x1 1.13 us: mix(): pl.pallas_call(mix_kernel, out_shape=jax.ShapeDtypeStruct(shape, jnp.bflo...]
where the time goes in v3:
time: 74.4 us; the launch traced here: 74.3 us
  blocking collectives  66.8 us (90%)
  Pallas kernels  7 us (9%)
    all_to_all x2, blocking collectives, exchange(): lax.all_to_all(pieces, ALL, split_axis=0, concat_axis=0, tiled=True)  66.8 us
    pallas_call x1, Pallas kernels, mlp(): pl.pallas_call(mlp_kernel, out_shape=jax.ShapeDtypeStruct((rows, width),...  3.72 us
    pallas_call x1, Pallas kernels, front(): pl.pallas_call(front_kernel, out_shape=(jax.ShapeDtypeStruct((2 * experts...  2.15 us

profile of v3, /device:TPU:1, one launch (start us, length us, event | category | flops | bytes accessed | tf_op | source)
XLA Modules:
  0.0 74.3 jit_solution(4439845321293213339)
XLA Ops:
  0.0 2.2 %front.1 = (bf16[256,2,640]{2,1,0:T(2,128)(2,1)S(1)}, bf16[256,256]{1,0:T(8,128)(2,1)S(1)}, f32[1,2560]{1,0:T(1,128)S(1)}, f32[1,1280]{1,0:T(1,128)S(1)}) custom-call(bf16[256,1280]{1,0:T(8,128)(2,1)} %bitcast.18, bf16[1280,128]{1,0:T(8,128)(2,1)} %r_hbm.1, bf16[1,5120]{1,0:T(2,128)(2,1)} %bi_hbm.1, bf16[1,1280]{1,0:T(2,128)(2,1)} %bo_hbm.1), custom_call_target="tpu_custom_call" | custom-call | tf_op jit(solution)/shard_map/front/pallas_call | solution.py:70
  2.2 0.0 slice-start
  2.2 0.0 slice-start.2
  2.2 0.0 slice-start.1
  2.2 0.0 slice-start.3
  2.2 38.1 %all_to_all.10 = bf16[256,2,640]{2,1,0:T(2,128)(2,1)S(1)} all-to-all(bf16[256,2,640]{2,1,0:T(2,128)(2,1)S(1)} %hold.3), channel_id=1, replica_groups=mesh['dp'=2,'expert'=128] {'dp','expert'}, dimensions={0} | all-to-all | bytes 1310720 | tf_op jit(solution)/shard_map/all_to_all | solution.py:166
  40.3 0.1 copy.9
  40.4 0.0 slice-done
  40.4 0.0 slice-done.2
  40.4 0.0 slice-done.1
  40.4 0.0 slice-done.3
  40.5 3.7 %mlp.1 = bf16[256,1280]{1,0:T(8,128)(2,1)S(1)} custom-call(bf16[256,1280]{1,0:T(8,128)(2,1)S(1)} %bitcast.15, f32[1,2560]{1,0:T(1,128)S(1)} %get-tuple-element.11.bias_ref, f32[1,1280]{1,0:T(1,128)S(1)} %get-tuple-element.12.share_ref, bf16[1280,2560]{1,0:T(8,128)(2,1)S(1)} %bitcast.10, bf16[2560,1280]{1,0:T(8,128)(2,1)S(1)} %bitcast.13), custom_call_target="tpu_custom_call" | custom-call | tf_op jit(solution)/shard_map/mlp/pallas_call | solution.py:105
  44.2 0.1 reshape.10
  44.3 28.8 %all_to_all.11 = bf16[256,2,640]{2,1,0:T(2,128)(2,1)S(1)} all-to-all(bf16[256,2,640]{2,1,0:T(2,128)(2,1)S(1)} %reshape.10), channel_id=1, replica_groups=mesh['dp'=2,'expert'=128] {'dp','expert'}, dimensions={0} | all-to-all | bytes 1310720 | tf_op jit(solution)/shard_map/all_to_all | solution.py:166
  73.1 0.1 copy.10
  73.2 1.1 %mix.1 = bf16[256,1280]{1,0:T(8,128)(2,1)} custom-call(bf16[256,256]{1,0:T(8,128)(2,1)S(1)} %get-tuple-element.9.w_ref, bf16[256,1280]{1,0:T(8,128)(2,1)S(1)} %bitcast.14), custom_call_target="tpu_custom_call" | custom-call | tf_op jit(solution)/shard_map/mix/pallas_call | solution.py:153
  (4 shorter events, 0.0 us)
Async XLA Ops:
  2.2 38.2 %slice-start = ((s8[6553600]{0:T(1024)(128)(4,1)}), s8[4194304]{0:T(1024)(128)(4,1)S(1)}, s32[]{:S(2)}) async-start(s8[6553600]{0:T(1024)(128)(4,1)} %bitcast.8), calls=%async_computation.2 | async-start | bytes 8388608
  2.2 38.2 %slice-start.2 = ((s8[6553600]{0:T(1024)(128)(4,1)}), s8[4194304]{0:T(1024)(128)(4,1)S(1)}, s32[]{:S(2)}) async-start(s8[6553600]{0:T(1024)(128)(4,1)} %bitcast.11), calls=%async_computation.4 | async-start | bytes 8388608
  2.2 38.2 %slice-start.1 = ((s8[6553600]{0:T(1024)(128)(4,1)}), s8[2359296]{0:T(1024)(128)(4,1)S(1)}, s32[]{:S(2)}) async-start(s8[6553600]{0:T(1024)(128)(4,1)} %bitcast.8), calls=%async_computation.3 | async-start | bytes 4718592
  2.2 38.2 %slice-start.3 = ((s8[6553600]{0:T(1024)(128)(4,1)}), s8[2359296]{0:T(1024)(128)(4,1)S(1)}, s32[]{:S(2)}) async-start(s8[6553600]{0:T(1024)(128)(4,1)} %bitcast.11), calls=%async_computation.5 | async-start | bytes 4718592

commit v4 on v3

--- a/solution.py
+++ b/solution.py
@@ -11,7 +11,7 @@
 
 EXPERT = ("expert",)
 ALL = ("dp", "expert")
-CHUNK = 512
+CHUNK = 1280
 GRANT = 8 << 20
 PARTS = 2
 HOLD_FLOPS = 20_000_000_000
@@ -37,6 +37,12 @@
     cr.start()
     ci.start()
     co.start()
+    ci.wait()
+    co.wait()
+    bias = bi_ref[...].astype(jnp.float32)
+    bias_ref[...] = jnp.where(half == 0, bias[:, :hid], bias[:, hid:])
+    share = bo_ref[...].astype(jnp.float32)
+    share_ref[...] = jnp.where(half == 0, share, jnp.zeros_like(share))
     cx.wait()
     cr.wait()
     x = x_ref[...]
@@ -56,12 +62,6 @@
     combine = (ex / jnp.sum(ex, axis=1, keepdims=True)).astype(jnp.bfloat16)
     comb_ref[:, :experts] = combine
     comb_ref[:, experts:] = combine
-    ci.wait()
-    co.wait()
-    bias = bi_ref[...].astype(jnp.float32)
-    bias_ref[...] = jnp.where(half == 0, bias[:, :hid], bias[:, hid:])
-    share = bo_ref[...].astype(jnp.float32)
-    share_ref[...] = jnp.where(half == 0, share, jnp.zeros_like(share))
 
 
 def front(x, router, b_in, b_out, hid):

time: 74.4 us -> 74.4 us (level)
  no operation moved by 1% of the time
where the time goes in v4:
time: 74.4 us; the launch traced here: 74.3 us
  blocking collectives  66.8 us (90%)
  Pallas kernels  6.99 us (9%)
    all_to_all x2, blocking collectives, exchange(): lax.all_to_all(pieces, ALL, split_axis=0, concat_axis=0, tiled=True)  66.8 us
    pallas_call x1, Pallas kernels, mlp(): pl.pallas_call(mlp_kernel, out_shape=jax.ShapeDtypeStruct((rows, width),...  3.72 us
    pallas_call x1, Pallas kernels, front(): pl.pallas_call(front_kernel, out_shape=(jax.ShapeDtypeStruct((2 * experts...  2.14 us

profile of v4, /device:TPU:1, one launch (start us, length us, event | category | flops | bytes accessed | tf_op | source)
XLA Modules:
  0.0 74.3 jit_solution(3192341999200765367)
XLA Ops:
  0.0 2.1 %front.1 = (bf16[256,2,640]{2,1,0:T(2,128)(2,1)S(1)}, bf16[256,256]{1,0:T(8,128)(2,1)S(1)}, f32[1,2560]{1,0:T(1,128)S(1)}, f32[1,1280]{1,0:T(1,128)S(1)}) custom-call(bf16[256,1280]{1,0:T(8,128)(2,1)} %bitcast.18, bf16[1280,128]{1,0:T(8,128)(2,1)} %r_hbm.1, bf16[1,5120]{1,0:T(2,128)(2,1)} %bi_hbm.1, bf16[1,1280]{1,0:T(2,128)(2,1)} %bo_hbm.1), custom_call_target="tpu_custom_call" | custom-call | tf_op jit(solution)/shard_map/front/pallas_call | solution.py:70
  2.1 0.0 slice-start
  2.2 0.0 slice-start.2
  2.2 0.0 slice-start.1
  2.2 0.0 slice-start.3
  2.2 38.1 %all_to_all.10 = bf16[256,2,640]{2,1,0:T(2,128)(2,1)S(1)} all-to-all(bf16[256,2,640]{2,1,0:T(2,128)(2,1)S(1)} %hold.3), channel_id=1, replica_groups=mesh['dp'=2,'expert'=128] {'dp','expert'}, dimensions={0} | all-to-all | bytes 1310720 | tf_op jit(solution)/shard_map/all_to_all | solution.py:166
  40.3 0.1 copy.9
  40.4 0.0 slice-done
  40.4 0.0 slice-done.2
  40.4 0.0 slice-done.1
  40.4 0.0 slice-done.3
  40.4 3.7 %mlp.1 = bf16[256,1280]{1,0:T(8,128)(2,1)S(1)} custom-call(bf16[256,1280]{1,0:T(8,128)(2,1)S(1)} %bitcast.15, f32[1,2560]{1,0:T(1,128)S(1)} %get-tuple-element.11.bias_ref, f32[1,1280]{1,0:T(1,128)S(1)} %get-tuple-element.12.share_ref, bf16[1280,2560]{1,0:T(8,128)(2,1)S(1)} %bitcast.10, bf16[2560,1280]{1,0:T(8,128)(2,1)S(1)} %bitcast.13), custom_call_target="tpu_custom_call" | custom-call | tf_op jit(solution)/shard_map/mlp/pallas_call | solution.py:105
  44.2 0.1 reshape.10
  44.3 28.8 %all_to_all.11 = bf16[256,2,640]{2,1,0:T(2,128)(2,1)S(1)} all-to-all(bf16[256,2,640]{2,1,0:T(2,128)(2,1)S(1)} %reshape.10), channel_id=1, replica_groups=mesh['dp'=2,'expert'=128] {'dp','expert'}, dimensions={0} | all-to-all | bytes 1310720 | tf_op jit(solution)/shard_map/all_to_all | solution.py:166
  73.1 0.1 copy.10
  73.2 1.1 %mix.1 = bf16[256,1280]{1,0:T(8,128)(2,1)} custom-call(bf16[256,256]{1,0:T(8,128)(2,1)S(1)} %get-tuple-element.9.w_ref, bf16[256,1280]{1,0:T(8,128)(2,1)S(1)} %bitcast.14), custom_call_target="tpu_custom_call" | custom-call | tf_op jit(solution)/shard_map/mix/pallas_call | solution.py:153
  (4 shorter events, 0.0 us)
Async XLA Ops:
  2.1 38.2 %slice-start = ((s8[6553600]{0:T(1024)(128)(4,1)}), s8[4194304]{0:T(1024)(128)(4,1)S(1)}, s32[]{:S(2)}) async-start(s8[6553600]{0:T(1024)(128)(4,1)} %bitcast.8), calls=%async_computation.2 | async-start | bytes 8388608
  2.2 38.2 %slice-start.2 = ((s8[6553600]{0:T(1024)(128)(4,1)}), s8[4194304]{0:T(1024)(128)(4,1)S(1)}, s32[]{:S(2)}) async-start(s8[6553600]{0:T(1024)(128)(4,1)} %bitcast.11), calls=%async_computation.4 | async-start | bytes 8388608
  2.2 38.2 %slice-start.1 = ((s8[6553600]{0:T(1024)(128)(4,1)}), s8[2359296]{0:T(1024)(128)(4,1)S(1)}, s32[]{:S(2)}) async-start(s8[6553600]{0:T(1024)(128)(4,1)} %bitcast.8), calls=%async_computation.3 | async-start | bytes 4718592
  2.2 38.2 %slice-start.3 = ((s8[6553600]{0:T(1024)(128)(4,1)}), s8[2359296]{0:T(1024)(128)(4,1)S(1)}, s32[]{:S(2)}) async-start(s8[6553600]{0:T(1024)(128)(4,1)} %bitcast.11), calls=%async_computation.5 | async-start | bytes 4718592
